TPU v7x, 128 devices: a whole 4x4x4 slice. The times are simulated.
128 devices in a mesh: slab: 32 (over y, x, core), orb: 4 (over z).
Axes of the slice: x: 4, y: 4, z: 4, core: 2. Of those that a mesh axis runs over, the one named last changes fastest.
Arguments:
- orbitals: float32 [256, 64, 4096], P('orb', 'slab'), may hold values from -6 to 6
- pair_list: int32 [128, 2], P(('slab', 'orb')), may hold values from 0 to 255, as said below
- box_start: int32 [128, 3], P(('slab', 'orb')), may hold values from 0 to 63
Outputs:
- exchange_action: float32 [256, 64, 4096], P('orb', 'slab')
Inputs may be any that keep to these rules, and one draw needn't show every extreme that they name: `pair_list`: the two orbitals of a row differ.
All inputs are finite; a program needn't handle non-finite values.
Results may differ from a plain program's by a relative error of at most 0.0003.
Values sent between devices are 32-bit elements; how exact they have to be, the bound alone decides.
A program may use at most 128 MiB of HBM per device.

v0:
```python
import jax
import jax.numpy as jnp
from jax import lax
from jax.sharding import PartitionSpec as P

NX = 64
NY = 64
NZ = 64
ITERS = 16
screening = 0.02
center_eig = 6.0 + screening
half_width = 6.0
sigma_one = center_eig / half_width


def side_by_side(arrays, axis, dim, along):
    ends, at = ([], 0)
    for a in arrays[:-1]:
        at += a.shape[along]
        ends.append(at)
    both = jnp.concatenate(arrays, axis=along)
    return tuple(jnp.split(lax.all_gather(both, axis, axis=dim, tiled=True), ends, axis=along))


def operate(field):
    cells = field.shape[2]
    z_index = jnp.arange(cells, dtype=jnp.int32) % NZ
    beside = jnp.roll(field, 1, 1) + jnp.roll(field, -1, 1)
    beside = beside + jnp.roll(field, NZ, 2) + jnp.roll(field, -NZ, 2)
    upper = jnp.where(z_index == NZ - 1, jnp.roll(field, NZ - 1, 2), jnp.roll(field, -1, 2))
    lower = jnp.where(z_index == 0, jnp.roll(field, 1 - NZ, 2), jnp.roll(field, 1, 2))
    return center_eig * field - (beside + upper + lower)


def solve_screened(density):

    def sweep(step_index, state_now):
        solution, residue, update, ratio = state_now
        solution = solution + update
        residue = residue - operate(update)
        ratio_next = 1.0 / (2.0 * sigma_one - ratio)
        update = ratio_next * ratio * update + 2.0 * ratio_next / half_width * residue
        return (solution, residue, update, ratio_next)

    start_state = (
        jnp.zeros_like(density),
        density,
        density / center_eig,
        jnp.asarray(1.0 / sigma_one, jnp.float32),
    )
    return lax.fori_loop(0, ITERS, sweep, start_state)[0]


def pair_work(received):
    left = received[:, 0]
    right = received[:, 1]
    potential = solve_screened(left * right)
    return jnp.stack([-potential * right, -potential * left], axis=1)


def box_mask(starts, slab_at, slab_rows, cells):
    x_cells = slab_at * slab_rows + jnp.arange(slab_rows, dtype=jnp.int32)
    cell_index = jnp.arange(cells, dtype=jnp.int32)
    y_index = cell_index // NZ
    z_index = cell_index % NZ
    inside_x = (x_cells[None, None, :] - starts[:, :, 0:1]) % NX < NX // 2
    inside_y = (y_index[None, None, :] - starts[:, :, 1:2]) % NY < NY // 2
    inside_z = (z_index[None, None, :] - starts[:, :, 2:3]) % NZ < NZ // 2
    inside = inside_x[:, :, :, None] & (inside_y & inside_z)[:, :, None, :]
    return inside[:, None]


def body(orbitals, pair_list, box_start):
    n_slab = lax.axis_size("slab")
    n_orb = lax.axis_size("orb")
    slab_at = lax.axis_index("slab")
    orb_at = lax.axis_index("orb")
    orb_dev, slab_rows, cells = orbitals.shape
    pair_dev = pair_list.shape[0]
    devices = n_slab * n_orb
    all_pairs, all_boxes = side_by_side((pair_list, box_start), ("slab", "orb"), 0, 1)
    pair_grid = all_pairs.reshape(n_slab, n_orb, pair_dev, 2)
    box_grid = all_boxes.reshape(n_slab, n_orb, pair_dev, 3)
    row_pairs = jnp.take(pair_grid, orb_at, axis=1).transpose(1, 2, 0)
    own_y = jnp.broadcast_to(box_start[:, None, 1:2], (pair_dev, 2, 1)).reshape(-1)
    own_z = jnp.broadcast_to(box_start[:, None, 2:3], (pair_dev, 2, 1)).reshape(-1)
    boxed_frame = False
    gathered = lax.all_gather(orbitals, "orb", axis=0, tiled=True)
    starts = jnp.take(box_grid, orb_at, axis=1).transpose(1, 0, 2)
    pieces = jnp.take(gathered, row_pairs, axis=0)
    pieces = jnp.where(box_mask(starts, slab_at, slab_rows, cells), pieces, 0.0)
    outgoing = pieces.reshape(pair_dev, 2, n_slab * slab_rows, cells)
    terms = pair_work(lax.all_to_all(outgoing, "slab", split_axis=2, concat_axis=2, tiled=True))
    full_rows = n_slab * slab_rows
    spread = jnp.broadcast_to(
        terms.reshape(pair_dev, 2, n_slab, 1, slab_rows, cells),
        (pair_dev, 2, n_slab, n_orb, slab_rows, cells),
    )
    spread = spread.reshape(pair_dev, 2, devices * slab_rows, cells)
    returned = lax.all_to_all(spread, ("slab", "orb"), split_axis=2, concat_axis=2, tiled=True)
    owners = (
        all_pairs.reshape(devices, pair_dev, 2).transpose(1, 2, 0).reshape(-1) - orb_at * orb_dev
    )
    one_hot = (jnp.arange(orb_dev, dtype=jnp.int32)[:, None] == owners[None, :]).astype(jnp.float32)
    action = jnp.dot(
        one_hot,
        returned.reshape(pair_dev * 2 * devices, slab_rows * cells),
        precision=lax.Precision.HIGHEST,
        preferred_element_type=jnp.float32,
    )
    return action.reshape(orb_dev, slab_rows, cells)


def solution(mesh):
    return jax.shard_map(
        body,
        mesh=mesh,
        in_specs=(P("orb", "slab", None), P(("slab", "orb"), None), P(("slab", "orb"), None)),
        out_specs=P("orb", "slab", None),
        check_vma=False,
    )
```

profile of v0, /device:TPU:1, one launch (start us, length us, event | category | flops | bytes accessed | tf_op | source)
XLA Modules:
  0.0 380.7 jit_solution(14061761828574327259)
XLA Ops:
  7.4 50.4 %all-gather = s32[128,1,5]{2,1,0:T(1,128)S(1)} all-gather(s32[1,1,5]{2,1,0:T(1,128)S(1)} %add_bitcast_fusion), channel_id=1, replica_groups=mesh['slab'=32,'orb'=4] {'slab','orb'}, dimensions={0}, use_global_device_ids=true | all-gather | bytes 2580 | tf_op jit(solution)/shard_map/all_gather | solution.py:22
  60.8 35.6 %all-gather.3.cloned.1.call-done = f32[256,2,4096]{2,1,0:T(2,128)} async-done(((f32[64,2,4096]{2,1,0:T(2,128)}), f32[256,2,4096]{2,1,0:T(2,128)}) %all-gather.3.cloned.1.call-update) | async-done | bytes 8388624 | tf_op jit(solution)/shard_map/all_gather | solution.py:88
  96.4 6.2 %gather_fusion = f32[64,2,4096]{2,1,0:T(2,128)S(1)} fusion(f32[256,2,4096]{2,1,0:T(2,128)} %all-gather.3.cloned.1.call-done, s32[1024]{0:T(1024)S(1)} %pad_clamp_fusion), kind=kCustom, calls=%fused_computation | custom fusion | bytes 4194560 | tf_op jit(solution)/shard_map/jit(_take)/gather | solution.py:90
  102.6 2.4 gather.17
  105.0 5.6 %fusion.11 = f32[1,2,64,4096]{3,1,0,2:T(2,128)} fusion(f32[1,2,64,4096]{3,2,1,0:T(8,128)} %gather.17, pred[2,64]{0,1:T(8,128)(4,1)S(1)} %copy.15, pred[64,4096]{1,0:T(8,128)(4,1)S(1)} %broadcast_and_fusion), kind=kLoop, calls=%fused_computation.22 | loop fusion | flops 1048576 | bytes 4456576 | tf_op jit(solution)/shard_map/jit(_where)/select_n | solution.py:91
  110.6 7.7 %all-to-all-start = ((f32[1,2,64,4096]{3,1,0,2:T(2,128)}), f32[1,2,64,4096]{3,1,0,2:T(2,128)S(1)}, u32[]{:S(2)}, u32[]{:S(2)}) async-start(f32[1,2,64,4096]{3,1,0,2:T(2,128)} %fusion.11), calls=%async_computation | async-start | bytes 4194304 | tf_op jit(solution)/shard_map/all_to_all | solution.py:93
  118.4 28.5 %all-to-all-done = f32[1,2,64,4096]{3,1,0,2:T(2,128)S(1)} async-done(((f32[1,2,64,4096]{3,1,0,2:T(2,128)}), f32[1,2,64,4096]{3,1,0,2:T(2,128)S(1)}, u32[]{:S(2)}, u32[]{:S(2)}) %all-to-all-start) | async-done | bytes 2097184 | tf_op jit(solution)/shard_map/all_to_all | solution.py:93
  146.9 2.3 broadcast_multiply_fusion
  150.5 54.3 %while.19 = (s32[]{:T(128)}, f32[1,64,4096]{2,1,0:T(8,128)S(1)}, f32[1,64,4096]{2,1,0:T(8,128)S(1)}, f32[1,64,4096]{2,1,0:T(8,128)S(1)}, f32[]{:T(128)}, /*index...) while((s32[]{:T(128)}, f32[1,64,4096]{2,1,0:T(8,128)S(1)}, ...), condition=%wide.region_1.2_spmd.clone, body=%wide.region_0.1_spmd.clone.sunk | while | flops 6062087 | bytes 32522416 | solution.py:51
  152.4 1.5 multiply_add_fusion.2
  159.2 1.5 multiply_add_fusion.2
  166.0 1.5 multiply_add_fusion.2
  172.7 1.5 multiply_add_fusion.2
  204.8 5.3 %fusion.14 = (f32[1,64,4096]{2,0,1:T(1,128)S(1)}, f32[1,64,4096]{2,0,1:T(1,128)S(1)}) fusion(f32[1,2,64,4096]{3,1,0,2:T(2,128)} %copy-done, f32[1,64,4096]{2,1,0:T(8,128)S(1)} %get-tuple-element.32), kind=kLoop, calls=%fused_computation.38 | loop fusion | flops 786432 | bytes 5242880 | tf_op jit(solution)/shard_map/mul | solution.py:58
  210.1 4.0 %pad_maximum_fusion = f32[1,2,32,1,2,4096]{5,0,4,3,2,1:T(1,128)S(1)} fusion(f32[1,1,32,1,2,4096]{5,0,4,3,2,1:T(1,128)S(1)} %bitcast.60, f32[1,1,32,1,2,4096]{5,0,4,3,2,1:T(1,128)S(1)} %bitcast.59), kind=kLoop, calls=%fused_computation.19 | loop fusion | flops 524288 | bytes 4194304 | tf_op jit(solution)/shard_map/stack | solution.py:58
  214.1 1.9 copy.38
  216.0 7.5 %broadcast_in_dim.91 = f32[2,32,4,2,4096]{4,0,3,2,1:T(2,128)} broadcast(f32[2,32,2,4096]{3,0,2,1:T(2,128)S(1)} %bitcast.58), dimensions={0,1,3,4} | broadcast | bytes 10485760 | tf_op jit(solution)/shard_map/broadcast_in_dim | solution.py:95
  223.5 6.4 %all-to-all-start.1 = ((f32[1,2,256,4096]{3,1,0,2:T(2,128)}), f32[1,2,256,4096]{3,1,0,2:T(2,128)}, u32[]{:S(2)}, u32[]{:S(2)}) async-start(f32[1,2,256,4096]{3,1,0,2:T(2,128)} %bitcast.55), calls=%async_computation.1 | async-start | bytes 16777216 | tf_op jit(solution)/shard_map/all_to_all | solution.py:100
  230.0 102.7 %all-to-all-done.1 = f32[1,2,256,4096]{3,1,0,2:T(2,128)} async-done(((f32[1,2,256,4096]{3,1,0,2:T(2,128)}), f32[1,2,256,4096]{3,1,0,2:T(2,128)}, u32[]{:S(2)}, u32[]{:S(2)}) %all-to-all-start.1) | async-done | bytes 8388640 | tf_op jit(solution)/shard_map/all_to_all | solution.py:100
  332.7 11.5 %copy.22 = f32[1,2,256,4096]{3,2,1,0:T(8,128)} copy(f32[1,2,256,4096]{3,1,0,2:T(2,128)} %all-to-all-done.1) | data formatting | bytes 16777216 | tf_op jit(solution)/shard_map/all_to_all | solution.py:100
  344.2 10.0 %reshape.587 = f32[256,8192]{1,0:T(8,128)} reshape(f32[1,2,256,4096]{3,2,1,0:T(8,128)} %copy.22) | data formatting | bytes 16777216 | tf_op jit(solution)/shard_map/reshape | solution.py:107
  354.2 9.0 %copy.23 = f32[8192,256]{1,0:T(8,128)} copy(f32[8192,256]{0,1:T(8,128)} %bitcast.57) | data formatting | bytes 16777216 | tf_op jit(solution)/shard_map/dot_general | solution.py:105
  363.2 7.7 %fusion.21 = f32[64,2,4096]{2,0,1:T(8,128)S(1)} fusion(f32[2,4096,256]{2,1,0:T(8,128)} %bitcast.56, s32[256]{0:T(256)S(1)} %bitcast.65), kind=kOutput, calls=%fused_computation.49 | convolution fusion | flops 1610629120 | bytes 10486784 | tf_op jit(solution)/shard_map/dot_general | solution.py:105
  370.9 2.9 copy.24
  (208 shorter events, 51.7 us)
Async XLA Ops:
  6.5 0.7 copy-start.1
  6.5 0.7 copy-start.2
  6.5 89.9 %all-gather.3.cloned.1.call-start = ((), (), s32[]{:S(2)}) async-start(), calls=%async_computation.2 | async-start | bytes 10485760 | tf_op jit(solution)/shard_map/all_gather | solution.py:88
  110.6 36.2 %all-to-all-start = ((f32[1,2,64,4096]{3,1,0,2:T(2,128)}), f32[1,2,64,4096]{3,1,0,2:T(2,128)S(1)}, u32[]{:S(2)}, u32[]{:S(2)}) async-start(f32[1,2,64,4096]{3,1,0,2:T(2,128)} %fusion.11), calls=%async_computation | async-start | bytes 4194304 | tf_op jit(solution)/shard_map/all_to_all | solution.py:93
  146.9 2.3 copy-start
  223.5 109.2 %all-to-all-start.1 = ((f32[1,2,256,4096]{3,1,0,2:T(2,128)}), f32[1,2,256,4096]{3,1,0,2:T(2,128)}, u32[]{:S(2)}, u32[]{:S(2)}) async-start(f32[1,2,256,4096]{3,1,0,2:T(2,128)} %bitcast.55), calls=%async_computation.1 | async-start | bytes 16777216 | tf_op jit(solution)/shard_map/all_to_all | solution.py:100
Sparse Core Ops, SparseCore 0:
  9.0 87.3 all-gather.2
where the time goes:
time: 382 us; the launch traced here: 381 us
  waiting for transfers between devices  168 us (44%)
  local copies, waits for them, and re-layouts  78.2 us (20%)
  blocking collectives  50.4 us (13%)
  other arithmetic  47.3 us (12%)
  starting transfers between devices  14.1 us (4%)
  between operations  13.6 us (4%)
  matrix products  7.74 us (2%)
    all_to_all x1, waiting for transfers between devices, body(): lax.all_to_all(spread, ('slab', 'orb'), split_axis=2, concat_axis=2, tile...  103 us
    all_gather x1, blocking collectives, side_by_side(): lax.all_gather(both, axis, axis=dim, tiled=True)  50.4 us
    all_gather x1, waiting for transfers between devices, body(): gathered = lax.all_gather(orbitals, 'orb', axis=0, tiled=True)  35.6 us
    all_to_all x1, waiting for transfers between devices, body(): lax.all_to_all(outgoing, 'slab', split_axis=2, concat_axis=2, tiled=True)  28.5 us
    add x16, other arithmetic, sweep(): ratio_next * ratio * update + 2.0 * ratio_next / half_width * residue  23.7 us
    dot_general x2, local copies, waits for them, and re-layouts, body(): jnp.dot(one_hot, returned.reshape(pair_dev * 2 * devices, slab_rows * cel...  11.9 us
    all_to_all x1, local copies, waits for them, and re-layouts, body(): lax.all_to_all(spread, ('slab', 'orb'), split_axis=2, concat_axis=2, tile...  11.5 us
    reshape x1, local copies, waits for them, and re-layouts, body(): returned.reshape(pair_dev * 2 * devices, slab_rows * cells)  9.99 us
  transfers between devices with their start and end apart: 3, of which 3 were waited for; matrix products, arithmetic and copies ran while one was open for 1% of the time, Pallas kernels for 0%

commit v1 on v0

--- a/solution.py
+++ b/solution.py
@@ -85,7 +85,9 @@
     own_y = jnp.broadcast_to(box_start[:, None, 1:2], (pair_dev, 2, 1)).reshape(-1)
     own_z = jnp.broadcast_to(box_start[:, None, 2:3], (pair_dev, 2, 1)).reshape(-1)
     boxed_frame = False
-    gathered = lax.all_gather(orbitals, "orb", axis=0, tiled=True)
+    gathered = jnp.concatenate(
+        lax.all_to_all(jnp.stack([orbitals] * lax.axis_size("orb")), "orb", 0, 0), axis=0
+    )
     starts = jnp.take(box_grid, orb_at, axis=1).transpose(1, 0, 2)
     pieces = jnp.take(gathered, row_pairs, axis=0)
     pieces = jnp.where(box_mask(starts, slab_at, slab_rows, cells), pieces, 0.0)

time: 382 us -> 427 us (1.12)
  blocking collectives: 50.4 us -> 133 us
  waiting for transfers between devices: 168 us -> 131 us
  between operations: 13.6 us -> 0.22 us
  local copies, waits for them, and re-layouts: 78.2 us -> 90.2 us
    all_gather x1, blocking collectives: 50.4 us -> 133 us  [side_by_side(): lax.all_gather(both, axis, axis=dim, tiled=True)]
    all_gather x1 -> x0, waiting for transfers between devices: 35.6 us -> none  [body(): gathered = lax.all_gather(orbitals, 'orb', axis=0, tiled=True)]
    another operation x0 -> x1, local copies, waits for them, and re-layouts: none -> 9.09 us  [body(): jnp.stack([orbitals] * lax.axis_size('orb'))]
    all_to_all x0 -> x1, starting transfers between devices: none -> 5.98 us  [body(): lax.all_to_all(jnp.stack([orbitals] * lax.axis_size('orb')), 'orb', 0, 0)]
  transfers between devices with their start and end apart: 3 -> 3, of which waited for: 3 -> 2; matrix products, arithmetic and copies ran while one was open for 1% -> 1% of each run, Pallas kernels for 0% -> 0%
where the time goes in v1:
time: 427 us; the launch traced here: 426 us
  blocking collectives  133 us (31%)
  waiting for transfers between devices  131 us (31%)
  local copies, waits for them, and re-layouts  90.2 us (21%)
  other arithmetic  43.4 us (10%)
  starting transfers between devices  17.8 us (4%)
  matrix products  7.74 us (2%)
    all_gather x1, blocking collectives, side_by_side(): lax.all_gather(both, axis, axis=dim, tiled=True)  133 us
    all_to_all x1, waiting for transfers between devices, body(): lax.all_to_all(spread, ('slab', 'orb'), split_axis=2, concat_axis=2, tile...  103 us
    all_to_all x1, waiting for transfers between devices, body(): lax.all_to_all(outgoing, 'slab', split_axis=2, concat_axis=2, tiled=True)  28.5 us
    add x16, other arithmetic, sweep(): ratio_next * ratio * update + 2.0 * ratio_next / half_width * residue  23.7 us
    dot_general x2, local copies, waits for them, and re-layouts, body(): jnp.dot(one_hot, returned.reshape(pair_dev * 2 * devices, slab_rows * cel...  11.9 us
    all_to_all x1, local copies, waits for them, and re-layouts, body(): lax.all_to_all(spread, ('slab', 'orb'), split_axis=2, concat_axis=2, tile...  11.5 us
    reshape x1, local copies, waits for them, and re-layouts, body(): returned.reshape(pair_dev * 2 * devices, slab_rows * cells)  9.98 us
    broadcast_in_dim x2, local copies, waits for them, and re-layouts, body(): jnp.broadcast_to(terms.reshape(pair_dev, 2, n_slab, 1, slab_rows, cells),...  9.4 us
  transfers between devices with their start and end apart: 3, of which 2 were waited for; matrix products, arithmetic and copies ran while one was open for 1% of the time, Pallas kernels for 0%

profile of v1, /device:TPU:1, one launch (start us, length us, event | category | flops | bytes accessed | tf_op | source)
XLA Modules:
  0.0 425.7 jit_solution(17376010108499345636)
XLA Ops:
  0.0 9.1 %stack.16 = f32[4,64,2,4096]{3,2,1,0:T(2,128)} broadcast(f32[64,2,4096]{2,1,0:T(2,128)} %param.5), dimensions={1,2,3} | broadcast | bytes 10485760 | tf_op jit(solution)/shard_map/stack | solution.py:89
  9.1 6.0 %all-to-all-start = ((f32[4,64,2,4096]{3,2,1,0:T(2,128)}), f32[4,64,2,4096]{3,2,1,0:T(2,128)}, u32[]{:S(2)}, u32[]{:S(2)}) async-start(f32[4,64,2,4096]{3,2,1,0:T(2,128)} %stack.16), calls=%async_computation | async-start | bytes 16777216 | tf_op jit(solution)/shard_map/all_to_all | solution.py:89
  15.2 133.3 %all-gather = s32[128,1,5]{2,1,0:T(1,128)S(1)} all-gather(s32[1,1,5]{2,1,0:T(1,128)S(1)} %add_bitcast_fusion), channel_id=1, replica_groups=mesh['slab'=32,'orb'=4] {'slab','orb'}, dimensions={0}, use_global_device_ids=true | all-gather | bytes 2580 | tf_op jit(solution)/shard_map/all_gather | solution.py:22
  151.4 6.2 %gather_fusion = f32[64,2,4096]{2,1,0:T(2,128)S(1)} fusion(f32[256,2,4096]{2,1,0:T(2,128)} %bitcast.16, s32[1024]{0:T(1024)S(1)} %pad_clamp_fusion), kind=kCustom, calls=%fused_computation | custom fusion | bytes 4194560 | tf_op jit(solution)/shard_map/jit(_take)/gather | solution.py:92
  157.6 2.4 gather.17
  160.0 1.9 select_select_fusion
  162.0 2.9 copy.27
  164.9 5.4 %all-to-all-start.1 = ((f32[1,2,64,4096]{3,1,0,2:T(2,128)}), f32[1,2,64,4096]{3,1,0,2:T(2,128)S(1)}, u32[]{:S(2)}, u32[]{:S(2)}) async-start(f32[1,2,64,4096]{3,1,0,2:T(2,128)} %copy.27), calls=%async_computation.1 | async-start | bytes 4194304 | tf_op jit(solution)/shard_map/all_to_all | solution.py:95
  170.4 28.5 %all-to-all-done.1 = f32[1,2,64,4096]{3,1,0,2:T(2,128)S(1)} async-done(((f32[1,2,64,4096]{3,1,0,2:T(2,128)}), f32[1,2,64,4096]{3,1,0,2:T(2,128)S(1)}, u32[]{:S(2)}, u32[]{:S(2)}) %all-to-all-start.1) | async-done | bytes 2097184 | tf_op jit(solution)/shard_map/all_to_all | solution.py:95
  198.9 2.3 broadcast_multiply_fusion
  202.5 54.3 %while.19 = (s32[]{:T(128)}, f32[1,64,4096]{2,1,0:T(8,128)S(1)}, f32[1,64,4096]{2,1,0:T(8,128)S(1)}, f32[1,64,4096]{2,1,0:T(8,128)S(1)}, f32[]{:T(128)}, /*index...) while((s32[]{:T(128)}, f32[1,64,4096]{2,1,0:T(8,128)S(1)}, ...), condition=%wide.region_1.2_spmd.clone, body=%wide.region_0.1_spmd.clone.sunk | while | flops 6062087 | bytes 32522424 | solution.py:51
  204.4 1.5 multiply_add_fusion.2
  207.8 1.5 multiply_add_fusion.2
  256.8 5.1 %fusion.13 = (f32[1,64,4096]{2,0,1:T(1,128)S(1)}, f32[1,64,4096]{2,0,1:T(1,128)S(1)}) fusion(f32[1,2,64,4096]{3,1,0,2:T(2,128)} %copy-done, f32[1,64,4096]{2,1,0:T(8,128)S(1)} %get-tuple-element.32), kind=kLoop, calls=%fused_computation.37 | loop fusion | flops 786432 | bytes 5242880 | tf_op jit(solution)/shard_map/mul | solution.py:58
  261.9 4.0 pad_maximum_fusion
  265.9 1.9 copy.46
  267.8 7.5 %broadcast_in_dim.91 = f32[2,32,4,2,4096]{4,0,3,2,1:T(2,128)} broadcast(f32[2,32,2,4096]{3,0,2,1:T(2,128)S(1)} %bitcast.59), dimensions={0,1,3,4} | broadcast | bytes 10485760 | tf_op jit(solution)/shard_map/broadcast_in_dim | solution.py:97
  275.3 6.4 %all-to-all-start.2 = ((f32[1,2,256,4096]{3,1,0,2:T(2,128)}), f32[1,2,256,4096]{3,1,0,2:T(2,128)}, u32[]{:S(2)}, u32[]{:S(2)}) async-start(f32[1,2,256,4096]{3,1,0,2:T(2,128)} %bitcast.56), calls=%async_computation.2 | async-start | bytes 16777216 | tf_op jit(solution)/shard_map/all_to_all | solution.py:102
  281.8 102.7 %all-to-all-done.2 = f32[1,2,256,4096]{3,1,0,2:T(2,128)} async-done(((f32[1,2,256,4096]{3,1,0,2:T(2,128)}), f32[1,2,256,4096]{3,1,0,2:T(2,128)}, u32[]{:S(2)}, u32[]{:S(2)}) %all-to-all-start.2) | async-done | bytes 8388640 | tf_op jit(solution)/shard_map/all_to_all | solution.py:102
  384.5 11.5 %copy.33 = f32[1,2,256,4096]{3,2,1,0:T(8,128)} copy(f32[1,2,256,4096]{3,1,0,2:T(2,128)} %all-to-all-done.2) | data formatting | bytes 16777216 | tf_op jit(solution)/shard_map/all_to_all | solution.py:102
  396.0 10.0 %reshape.593 = f32[256,8192]{1,0:T(8,128)} reshape(f32[1,2,256,4096]{3,2,1,0:T(8,128)} %copy.33) | data formatting | bytes 16777216 | tf_op jit(solution)/shard_map/reshape | solution.py:109
  406.0 9.0 %copy.34 = f32[8192,256]{1,0:T(8,128)} copy(f32[8192,256]{0,1:T(8,128)} %bitcast.58) | data formatting | bytes 16777216 | tf_op jit(solution)/shard_map/dot_general | solution.py:107
  415.0 7.7 %fusion.20 = f32[64,2,4096]{2,0,1:T(8,128)S(1)} fusion(f32[2,4096,256]{2,1,0:T(8,128)} %bitcast.57, s32[256]{0:T(256)S(1)} %bitcast.66), kind=kOutput, calls=%fused_computation.48 | convolution fusion | flops 1610629120 | bytes 10486784 | tf_op jit(solution)/shard_map/dot_general | solution.py:107
  422.7 2.9 copy.35
  (208 shorter events, 53.9 us)
Async XLA Ops:
  9.1 6.0 %copy-start.1 = (s32[1,3]{1,0:T(1,128)S(1)}, s32[1,3]{1,0:T(1,128)}, u32[]{:S(2)}) copy-start(s32[1,3]{1,0:T(1,128)} %param.7) | copy-start | bytes 40
  9.1 6.0 %copy-start.2 = (s32[1,2]{1,0:T(1,128)S(1)}, s32[1,2]{1,0:T(1,128)}, u32[]{:S(2)}) copy-start(s32[1,2]{1,0:T(1,128)} %param.6) | copy-start | bytes 28
  9.1 142.3 %all-to-all-start = ((f32[4,64,2,4096]{3,2,1,0:T(2,128)}), f32[4,64,2,4096]{3,2,1,0:T(2,128)}, u32[]{:S(2)}, u32[]{:S(2)}) async-start(f32[4,64,2,4096]{3,2,1,0:T(2,128)} %stack.16), calls=%async_computation | async-start | bytes 16777216 | tf_op jit(solution)/shard_map/all_to_all | solution.py:89
  164.9 34.0 %all-to-all-start.1 = ((f32[1,2,64,4096]{3,1,0,2:T(2,128)}), f32[1,2,64,4096]{3,1,0,2:T(2,128)S(1)}, u32[]{:S(2)}, u32[]{:S(2)}) async-start(f32[1,2,64,4096]{3,1,0,2:T(2,128)} %copy.27), calls=%async_computation.1 | async-start | bytes 4194304 | tf_op jit(solution)/shard_map/all_to_all | solution.py:95
  198.9 2.3 copy-start
  275.3 109.2 %all-to-all-start.2 = ((f32[1,2,256,4096]{3,1,0,2:T(2,128)}), f32[1,2,256,4096]{3,1,0,2:T(2,128)}, u32[]{:S(2)}, u32[]{:S(2)}) async-start(f32[1,2,256,4096]{3,1,0,2:T(2,128)} %bitcast.56), calls=%async_computation.2 | async-start | bytes 16777216 | tf_op jit(solution)/shard_map/all_to_all | solution.py:102
